TPU v7x, 32 devices: a whole 2x2x4 slice. The times are simulated.
32 devices in a mesh: dp: 2 (over x), expert: 4 (over z), tensor: 4 (over y, core).
Axes of the slice: x: 2, y: 2, z: 4, core: 2. Of those that a mesh axis runs over, the one named last changes fastest.
Arguments:
- tokens: bfloat16 [256, 3072], P(('dp', 'expert', 'tensor')), parts along dimension 0, may hold values from -6 to 6
- expert_ids: int32 [256, 2], P(('dp', 'expert', 'tensor')), parts along dimension 0, may hold values from 0 to 3, all different within a row; in each aligned block of 8 rows (0 to 7, 8 to 15, ...) at most 8 rows name the same one
- gate_weights: float32 [256, 2], P(('dp', 'expert', 'tensor')), parts along dimension 0, may hold values from 0.2 to 1
- gate_proj: bfloat16 [4, 3072, 8192], P('expert', None, 'tensor'), may hold values from -0.109375 to 0.109375
- up_proj: bfloat16 [4, 3072, 8192], P('expert', None, 'tensor'), may hold values from -0.109375 to 0.109375
- down_proj: bfloat16 [4, 8192, 3072], P('expert', 'tensor'), may hold values from -0.0625 to 0.0625
Outputs:
- mixture: bfloat16 [256, 3072], P(('dp', 'expert', 'tensor')), parts along dimension 0
There are 2 independent parts, one for each index of `dp`. A program takes and returns all parts, laid end to end along the dimension named above; an argument that names none is the same for every part. Nothing has to cross between parts.
Inputs may be any that keep to these rules, and one draw needn't show every extreme that they name: `expert_ids`: each token names two different experts; no expert is named by more than 8 tokens of one device (aligned blocks of 8 rows), and some blocks reach this bound.
All inputs are finite; a program needn't handle non-finite values.
Results may differ from a plain program's by a relative error of at most 0.015.
Values may be sent and summed in bfloat16 or wider, within the bound.
A program may use at most 64 MiB of HBM per device.

v0:
```python
import jax
import jax.numpy as jnp
from jax import lax
from jax.sharding import PartitionSpec as P


def expert_rows(rows, w_gate, w_up, w_down):
    width = rows.shape[-1]
    flat = rows.reshape(-1, width)
    gate = jnp.dot(flat, w_gate, preferred_element_type=jnp.float32)
    upward = jnp.dot(flat, w_up, preferred_element_type=jnp.float32)
    hidden = (jax.nn.silu(gate) * upward).astype(jnp.bfloat16)
    output = jnp.dot(hidden, w_down, preferred_element_type=jnp.float32).astype(jnp.bfloat16)
    return output.reshape(rows.shape[:-1] + (w_down.shape[1],))


def on_device(tokens, expert_ids, gate_weights, gate_proj, up_proj, down_proj):
    experts = lax.axis_size("expert")
    tensors = lax.axis_size("tensor")
    local_rows, width = tokens.shape
    capacity = min(local_rows, 4 * local_rows // experts)
    w_gate = gate_proj[0]
    w_up = up_proj[0]
    w_down = down_proj[0]
    flat_ids = expert_ids.reshape(-1)
    onehot = (flat_ids[:, None] == jnp.arange(experts, dtype=jnp.int32)[None, :]).astype(jnp.int32)
    earlier = jnp.cumsum(onehot, axis=0) - onehot
    slots = jnp.sum(onehot * earlier, axis=1)
    target = flat_ids * capacity + slots
    placed = target[:, None] == jnp.arange(experts * capacity, dtype=jnp.int32)[None, :]
    doubled = jnp.repeat(tokens, 2, axis=0)
    outgoing = jnp.dot(placed.astype(jnp.bfloat16).T, doubled, preferred_element_type=jnp.float32)
    outgoing = outgoing.astype(jnp.bfloat16).reshape(experts, capacity, width)
    arrived = lax.all_to_all(outgoing, "expert", split_axis=0, concat_axis=0, tiled=True)
    partials = expert_rows(
        lax.all_gather(arrived[:, None], "tensor", axis=1, tiled=True), w_gate, w_up, w_down
    )
    returned = lax.all_to_all(
        partials.reshape(experts * tensors, capacity, width),
        ("expert", "tensor"),
        split_axis=0,
        concat_axis=0,
        tiled=True,
    )
    results = jnp.sum(
        returned.reshape(experts, tensors, capacity, width).astype(jnp.float32), axis=1
    ).astype(jnp.bfloat16)
    weights = placed.astype(jnp.float32) * gate_weights.reshape(-1)[:, None]
    contrib = jnp.dot(
        weights,
        results.reshape(experts * capacity, width).astype(jnp.float32),
        precision=lax.Precision.HIGHEST,
    )
    return contrib.reshape(local_rows, 2, width).sum(axis=1).astype(jnp.bfloat16)


def solution(mesh):
    return jax.shard_map(
        on_device,
        mesh=mesh,
        in_specs=(
            P(("dp", "expert", "tensor"), None),
            P(("dp", "expert", "tensor"), None),
            P(("dp", "expert", "tensor"), None),
            P("expert", None, "tensor"),
            P("expert", None, "tensor"),
            P("expert", "tensor", None),
        ),
        out_specs=P(("dp", "expert", "tensor"), None),
        check_vma=False,
    )
```

profile of v0, /device:TPU:0, one launch (start us, length us, event | category | flops | bytes accessed | tf_op | source)
XLA Modules:
  0.0 67.2 jit_solution(17757227761435476865)
XLA Ops:
  0.0 0.8 %copy.10 = s32[8,2]{1,0:T(8,128)S(1)} copy(s32[8,2]{0,1:T(2,128)} %param.7) | data formatting | bytes 128 | tf_op args[1]
  0.8 0.1 eq.48
  0.8 0.1 fusion.25
  0.9 0.2 select_reduce_fusion
  1.1 0.9 %broadcast_in_dim.4 = bf16[8,2,3072]{2,1,0:T(2,128)(2,1)S(1)} broadcast(bf16[8,3072]{1,0:T(8,128)(2,1)} %param.6), dimensions={0,2} | broadcast | bytes 147456 | tf_op jit(solution)/shard_map/broadcast_in_dim | solution.py:31
  2.0 0.3 fusion.12
  2.4 13.6 %all_to_all.10 = bf16[4,8,3072]{2,1,0:T(8,128)(2,1)S(1)} all-to-all(bf16[4,8,3072]{2,1,0:T(8,128)(2,1)S(1)} %fusion.12), channel_id=1, replica_groups=mesh['dp'=2,'expert'=4,'tensor'=4] {'expert'}, dimensions={0} | all-to-all | bytes 393216 | tf_op jit(solution)/shard_map/all_to_all | solution.py:34
  16.0 8.6 %all-gather = bf16[4,32,3072]{2,1,0:T(8,128)(2,1)S(1)} all-gather(bf16[4,8,3072]{2,1,0:T(8,128)(2,1)S(1)} %all_to_all.10), channel_id=2, replica_groups=mesh['dp'=2,'expert'=4,'tensor'=4] {'tensor'}, dimensions={1}, use_global_device_ids=true | all-gather | bytes 983040 | tf_op jit(solution)/shard_map/all_gather | solution.py:36
  24.6 6.4 %fusion.4 = f32[128,2048]{1,0:T(8,128)S(1)} fusion(bf16[128,3072]{1,0:T(8,128)(2,1)S(1)} %bitcast.37, bf16[1,3072,2048]{2,1,0:T(8,128)(2,1)} %param.9), kind=kOutput, calls=%fused_computation.4 | convolution fusion | flops 1610612736 | bytes 14417920 | tf_op jit(solution)/shard_map/dot_general | solution.py:10
  31.0 0.0 copy-start
  31.0 12.9 %fusion.9 = bf16[16,8,3072]{2,1,0:T(8,128)(2,1)} fusion(bf16[1,2048,3072]{2,1,0:T(8,128)(2,1)} %param.11, bf16[128,3072]{1,0:T(8,128)(2,1)S(1)} %bitcast.38, bf16[1,3072,2048]{2,1,0:T(8,128)(2,1)} %param.10, f32[128,2048]{1,0:T(8,128)S(1)} %fusion.4), kind=kOutput, calls=%fused_computation.7 | convolution fusion | flops 3223191552 | bytes 27787264 | tf_op jit(solution)/shard_map/dot_general | solution.py:13
  43.9 3.6 %all-to-all-start.1 = ((bf16[16,8,3072]{2,1,0:T(8,128)(2,1)}), bf16[16,8,3072]{2,1,0:T(8,128)(2,1)S(1)}, u32[]{:S(2)}, u32[]{:S(2)}) async-start(bf16[16,8,3072]{2,1,0:T(8,128)(2,1)} %fusion.9), calls=%async_computation.1 | async-start | bytes 1572864 | tf_op jit(solution)/shard_map/all_to_all | solution.py:38
  47.5 0.1 reduce_sum.33
  47.6 0.1 copy.12
  47.7 18.5 %all-to-all-done.1 = bf16[16,8,3072]{2,1,0:T(8,128)(2,1)S(1)} async-done(((bf16[16,8,3072]{2,1,0:T(8,128)(2,1)}), bf16[16,8,3072]{2,1,0:T(8,128)(2,1)S(1)}, u32[]{:S(2)}, u32[]{:S(2)}) %all-to-all-start.1) | async-done | bytes 786464 | tf_op jit(solution)/shard_map/all_to_all | solution.py:38
  66.2 0.1 bitcast_reduce_fusion
  66.3 0.0 copy-done
  66.3 0.9 %convolution_reduce_fusion = bf16[8,3072]{1,0:T(8,128)(2,1)} fusion(bf16[4,8,3072]{2,1,0:T(8,128)(2,1)S(1)} %bitcast_reduce_fusion, f32[8,2]{0,1:T(2,128)S(1)} %copy-done, s32[8,2]{0,1:T(2,128)S(1)} %copy.12), kind=kOutput, calls=%fused_computation.12 | convolution fusion | flops 18899968 | bytes 245888 | tf_op jit(solution)/shard_map/dot_general | solution.py:49
  (4 shorter events, 0.1 us)
Async XLA Ops:
  31.0 35.3 %copy-start = (f32[8,2]{0,1:T(2,128)S(1)}, f32[8,2]{0,1:T(2,128)}, u32[]{:S(2)}) copy-start(f32[8,2]{0,1:T(2,128)} %param.8) | copy-start | bytes 196
  43.9 22.3 %all-to-all-start.1 = ((bf16[16,8,3072]{2,1,0:T(8,128)(2,1)}), bf16[16,8,3072]{2,1,0:T(8,128)(2,1)S(1)}, u32[]{:S(2)}, u32[]{:S(2)}) async-start(bf16[16,8,3072]{2,1,0:T(8,128)(2,1)} %fusion.9), calls=%async_computation.1 | async-start | bytes 1572864 | tf_op jit(solution)/shard_map/all_to_all | solution.py:38
where the time goes:
time: 67.6 us; the launch traced here: 67.2 us
  blocking collectives  22.2 us (33%)
  matrix products  20.5 us (30%)
  waiting for transfers between devices  18.5 us (27%)
  starting transfers between devices  3.61 us (5%)
  local copies, waits for them, and re-layouts  1.9 us (3%)
    all_to_all x1, waiting for transfers between devices, on_device(): lax.all_to_all(partials.reshape(experts * tensors, capacity, width), ('ex...  18.5 us
    all_to_all x1, blocking collectives, on_device(): lax.all_to_all(outgoing, 'expert', split_axis=0, concat_axis=0, tiled=True)  13.6 us
    dot_general x1, matrix products, expert_rows(): jnp.dot(hidden, w_down, preferred_element_type=jnp.float32)  12.9 us
    all_gather x1, blocking collectives, on_device(): lax.all_gather(arrived[:, None], 'tensor', axis=1, tiled=True)  8.6 us
    dot_general x1, matrix products, expert_rows(): gate = jnp.dot(flat, w_gate, preferred_element_type=jnp.float32)  6.41 us
    all_to_all x1, starting transfers between devices, on_device(): lax.all_to_all(partials.reshape(experts * tensors, capacity, width), ('ex...  3.61 us
  transfers between devices with their start and end apart: 1, of which 1 were waited for; matrix products, arithmetic and copies ran while one was open for 0% of the time, Pallas kernels for 0%

commit v1 on v0

v1 whole, which is shorter than its diff:
```python
import functools

import jax
import jax.numpy as jnp
from jax import lax
from jax.experimental import pallas as pl
from jax.experimental.pallas import tpu as pltpu
from jax.sharding import PartitionSpec as P

F32 = jnp.float32
BF16 = jnp.bfloat16
LANES = 128
MESH = pl.DeviceIdType.MESH


def chunk_width(total, most):
    width = most
    while total % width:
        width -= LANES
    return width


def layer(n_e, n_y, tok_ref, ids_ref, gw_ref, gate_ref, up_ref, down_ref, out_ref,
          xb, x, wts, hid, wg, wu, wd, part, core_in, mid, y_in, fin, z_in,
          tok_sem, g_sem, u_sem, d_sem,
          agz_s, agz_r, agy_s, agy_r, agc_s, agc_r,
          rc_s, rc_r, ry_s, ry_r, rz_s, rz_r):
    e = lax.axis_index("expert")
    t = lax.axis_index("tensor")
    y = t // 2
    c = t % 2
    rows, width = x.shape
    n_f, _, f_w = wg.shape
    n_d, _, d_w = wd.shape

    def slot(cc, yy, ee):
        return (cc * n_y + yy) * n_e + ee

    me = slot(c, y, e)
    others_e = [(e + k) % n_e for k in range(1, n_e)]
    others_y = [(y + k) % n_y for k in range(1, n_y)]
    partner = {"tensor": y * 2 + 1 - c}

    tok = pltpu.make_async_copy(tok_ref, xb.at[me, :, pl.ds(0, width)], tok_sem)
    tok.start()
    barrier = pltpu.get_barrier_semaphore()
    pl.semaphore_signal(barrier, inc=1, device_id=partner, device_id_type=MESH)
    for yy in others_y:
        pl.semaphore_signal(barrier, inc=1, device_id={"tensor": yy * 2 + c}, device_id_type=MESH)
    for ee in others_e:
        pl.semaphore_signal(barrier, inc=1, device_id={"expert": ee}, device_id_type=MESH)

    lane = lax.broadcasted_iota(jnp.int32, (ids_ref.shape[0], LANES), 1)
    ids = ids_ref[...]
    gw = gw_ref[...]
    w = jnp.where(ids[:, 0:1] == lane, gw[:, 0:1], 0.0) + jnp.where(ids[:, 1:2] == lane, gw[:, 1:2], 0.0)
    head = w.astype(BF16)
    xb[me, :, pl.ds(width, LANES)] = head
    xb[me, :, pl.ds(width + LANES, LANES)] = (w - head.astype(F32)).astype(BF16)
    tok.wait()
    pl.semaphore_wait(barrier, 1 + len(others_y) + len(others_e))

    def gather(index, send, recv, device):
        return pltpu.make_async_remote_copy(
            src_ref=xb.at[index], dst_ref=xb.at[index], send_sem=send, recv_sem=recv,
            device_id=device, device_id_type=MESH)

    sends = []

    def start(copy):
        copy.start()
        sends.append(copy)

    def weights(i):
        return (pltpu.make_async_copy(gate_ref.at[0, :, pl.ds(i * f_w, f_w)], wg.at[i], g_sem.at[i]),
                pltpu.make_async_copy(up_ref.at[0, :, pl.ds(i * f_w, f_w)], wu.at[i], u_sem.at[i]))

    def down(i):
        return pltpu.make_async_copy(down_ref.at[0, :, pl.ds(i * d_w, d_w)], wd.at[i], d_sem.at[i])

    for k, ee in enumerate(others_e):
        start(gather(me, agz_s.at[k], agz_r.at[k], {"expert": ee}))
    for k, yy in enumerate(others_y):
        start(gather(me, agy_s.at[k, 0], agy_r.at[k, 0], {"tensor": yy * 2 + c}))
    start(gather(me, agc_s.at[0, 0], agc_r.at[0, 0], partner))
    for i in range(n_f):
        for copy in weights(i):
            copy.start()
    for i in range(n_d):
        down(i).start()

    for k in range(1, n_e):
        source = slot(c, y, (e + n_e - k) % n_e)
        gather(source, agz_s.at[k - 1], agz_r.at[k - 1], {"expert": e}).wait_recv()
        for m, yy in enumerate(others_y):
            start(gather(source, agy_s.at[m, k], agy_r.at[m, k], {"tensor": yy * 2 + c}))
        start(gather(source, agc_s.at[0, k], agc_r.at[0, k], partner))
    for k in range(n_e):
        for m in range(1, n_y):
            source = slot(c, (y + n_y - m) % n_y, (e + n_e - k) % n_e)
            gather(source, agy_s.at[m - 1, k], agy_r.at[m - 1, k], partner).wait_recv()
            start(gather(source, agc_s.at[m, k], agc_r.at[m, k], partner))
    for k in range(n_e):
        for m in range(n_y):
            source = slot(1 - c, (y + n_y - m) % n_y, (e + n_e - k) % n_e)
            gather(source, agc_s.at[m, k], agc_r.at[m, k], partner).wait_recv()

    expert_lane = lax.broadcasted_iota(jnp.int32, (16, LANES), 1) == e

    def gathered(j, carry):
        pair = xb[pl.ds(2 * j, 2)].astype(F32).reshape(16, width + 2 * LANES)
        at = pl.ds(pl.multiple_of(16 * j, 16), 16)
        x[at, :] = pair[:, :width].astype(BF16)
        both = pair[:, width:width + LANES] + pair[:, width + LANES:]
        own = jnp.sum(jnp.where(expert_lane, both, 0.0), axis=1, keepdims=True)
        wts[at, :] = jnp.broadcast_to(own, (16, LANES))
        return carry

    lax.fori_loop(0, rows // 16, gathered, 0)

    def hidden(i, carry):
        pltpu.make_async_copy(gate_ref.at[0, :, pl.ds(0, f_w)], wg.at[i], g_sem.at[i]).wait()
        gate = jnp.dot(x[...], wg[i], preferred_element_type=F32)
        pltpu.make_async_copy(up_ref.at[0, :, pl.ds(0, f_w)], wu.at[i], u_sem.at[i]).wait()
        up = jnp.dot(x[...], wu[i], preferred_element_type=F32)
        value = gate / (1.0 + jnp.exp(-gate)) * up * wts[:, 0:1]
        hid[:, pl.ds(pl.multiple_of(i * f_w, LANES), f_w)] = value.astype(BF16)
        return carry

    lax.fori_loop(0, n_f, hidden, 0)

    def core_copy(i):
        return pltpu.make_async_remote_copy(
            src_ref=part.at[i, 1 - c], dst_ref=core_in.at[i], send_sem=rc_s.at[i], recv_sem=rc_r.at[i],
            device_id=partner, device_id_type=MESH)

    def y_copy(i, k, yy):
        return pltpu.make_async_remote_copy(
            src_ref=mid.at[i, yy], dst_ref=y_in.at[i, k], send_sem=ry_s.at[i, k], recv_sem=ry_r.at[i, k],
            device_id={"tensor": yy * 2 + c}, device_id_type=MESH)

    def z_copy(i, k, ee):
        return pltpu.make_async_remote_copy(
            src_ref=fin.at[i, ee], dst_ref=z_in.at[i, k], send_sem=rz_s.at[i, k], recv_sem=rz_r.at[i, k],
            device_id={"expert": ee}, device_id_type=MESH)

    def produce(i):
        down(i).wait()
        value = jnp.dot(hid[...], wd[i], preferred_element_type=F32)
        part[i] = value.reshape(
            part.shape[1:]).astype(BF16)
        start(core_copy(i))

    def over_cores(i):
        core_copy(i).wait_recv()
        mid[i] = (part[i, c].astype(F32) + core_in[i].astype(F32)).astype(BF16)
        for k, yy in enumerate(others_y):
            start(y_copy(i, k, yy))

    def over_y(i):
        total = mid[i, y].astype(F32)
        for k, yy in enumerate(others_y):
            y_copy(i, k, yy).wait_recv()
            total = total + y_in[i, k].astype(F32)
        fin[i] = total.astype(BF16)
        for k, ee in enumerate(others_e):
            start(z_copy(i, k, ee))

    def over_e(i):
        total = fin[i, e].astype(F32)
        for k, ee in enumerate(others_e):
            z_copy(i, k, ee).wait_recv()
            total = total + z_in[i, k].astype(F32)
        out_ref[:, pl.ds(i * d_w, d_w)] = total.astype(BF16)

    lags = ((produce, 0), (over_cores, 2), (over_y, 5), (over_e, 9))
    for step in range(n_d + lags[-1][1]):
        for stage, lag in lags:
            if 0 <= step - lag < n_d:
                stage(step - lag)
    for copy in sends:
        copy.wait_send()


def on_device(tokens, expert_ids, gate_weights, gate_proj, up_proj, down_proj):
    n_e = lax.axis_size("expert")
    n_t = lax.axis_size("tensor")
    n_y = n_t // 2
    local, width = tokens.shape
    ff = gate_proj.shape[2]
    rows = n_e * n_t * local
    f_w = chunk_width(ff, 512)
    d_w = chunk_width(width, 512)
    n_f, n_d = ff // f_w, width // d_w
    hbm = pl.BlockSpec(memory_space=pl.ANY)
    vmem = pl.BlockSpec(memory_space=pltpu.VMEM)
    dma = pltpu.SemaphoreType.DMA
    return pl.pallas_call(
        functools.partial(layer, n_e, n_y),
        out_shape=jax.ShapeDtypeStruct((local, width), BF16),
        in_specs=[hbm, vmem, vmem, hbm, hbm, hbm],
        out_specs=vmem,
        scratch_shapes=[
            pltpu.VMEM((n_e * n_t, local, width + 2 * LANES), BF16),
            pltpu.VMEM((rows, width), BF16),
            pltpu.VMEM((rows, LANES), F32),
            pltpu.VMEM((rows, ff), BF16),
            pltpu.VMEM((n_f, width, f_w), BF16),
            pltpu.VMEM((n_f, width, f_w), BF16),
            pltpu.VMEM((n_d, ff, d_w), BF16),
            pltpu.VMEM((n_d, 2, n_y, n_e, local, d_w), BF16),
            pltpu.VMEM((n_d, n_y, n_e, local, d_w), BF16),
            pltpu.VMEM((n_d, n_y, n_e, local, d_w), BF16),
            pltpu.VMEM((n_d, max(1, n_y - 1), n_e, local, d_w), BF16),
            pltpu.VMEM((n_d, n_e, local, d_w), BF16),
            pltpu.VMEM((n_d, max(1, n_e - 1), local, d_w), BF16),
            dma, dma((n_f,)), dma((n_f,)), dma((n_d,)),
            dma((n_e,)), dma((n_e,)),
            dma((n_y, n_e)), dma((n_y, n_e)),
            dma((n_y, n_e)), dma((n_y, n_e)),
            dma((n_d,)), dma((n_d,)),
            dma((n_d, n_y)), dma((n_d, n_y)),
            dma((n_d, n_e)), dma((n_d, n_e)),
        ],
        compiler_params=pltpu.CompilerParams(
            collective_id=0, has_side_effects=True, vmem_limit_bytes=64000 * 1024),
    )(tokens, expert_ids, gate_weights, gate_proj, up_proj, down_proj)


def solution(mesh):
    return jax.shard_map(
        on_device,
        mesh=mesh,
        in_specs=(
            P(("dp", "expert", "tensor"), None),
            P(("dp", "expert", "tensor"), None),
            P(("dp", "expert", "tensor"), None),
            P("expert", None, "tensor"),
            P("expert", None, "tensor"),
            P("expert", "tensor", None),
        ),
        out_specs=P(("dp", "expert", "tensor"), None),
        check_vma=False,
    )
```

time: 67.6 us -> 40.5 us (0.60)
  Pallas kernels: 0 us -> 36.1 us
  blocking collectives: 22.2 us -> 0 us
  matrix products: 20.5 us -> 0 us
  waiting for transfers between devices: 18.5 us -> 0 us
  starting transfers between devices: 3.61 us -> 0 us
  local copies, waits for them, and re-layouts: 1.9 us -> 4.11 us
    pallas_call x0 -> x1, Pallas kernels: none -> 36.1 us  [on_device(): pl.pallas_call(functools.partial(layer, n_e, n_y), out_shape=jax.ShapeDty...]
    dot_general x4 -> x0, matrix products: 20.5 us -> none  [the longest x1 12.9 us: expert_rows(): jnp.dot(hidden, w_down, preferred_element_type=jnp.float32)]
    all_to_all x1 -> x0, waiting for transfers between devices: 18.5 us -> none  [on_device(): lax.all_to_all(partials.reshape(experts * tensors, capacity, width), ('ex...]
    all_to_all x1 -> x0, blocking collectives: 13.6 us -> none  [on_device(): lax.all_to_all(outgoing, 'expert', split_axis=0, concat_axis=0, tiled=True)]
    all_gather x1 -> x0, blocking collectives: 8.6 us -> none  [on_device(): lax.all_gather(arrived[:, None], 'tensor', axis=1, tiled=True)]
    all_to_all x1 -> x0, starting transfers between devices: 3.61 us -> none  [on_device(): lax.all_to_all(partials.reshape(experts * tensors, capacity, width), ('ex...]
    unnamed x3, local copies, waits for them, and re-layouts: 0.76 us -> 4.11 us
    broadcast_in_dim x1 -> x0, local copies, waits for them, and re-layouts: 0.86 us -> none  [on_device(): doubled = jnp.repeat(tokens, 2, axis=0)]
  transfers between devices with their start and end apart: 1 -> 0, of which waited for: 1 -> 0; matrix products, arithmetic and copies ran while one was open for 0% -> 0% of each run, Pallas kernels for 0% -> 0%
where the time goes in v1:
time: 40.5 us; the launch traced here: 40.2 us
  Pallas kernels  36.1 us (89%)
  local copies, waits for them, and re-layouts  4.11 us (10%)
    pallas_call x1, Pallas kernels, on_device(): pl.pallas_call(functools.partial(layer, n_e, n_y), out_shape=jax.ShapeDty...  36.1 us
    unnamed x3, local copies, waits for them, and re-layouts  4.11 us

profile of v1, /device:TPU:0, one launch (start us, length us, event | category | flops | bytes accessed | tf_op | source)
XLA Modules:
  0.0 40.2 jit_solution(1953997281159880216)
XLA Ops:
  0.0 1.3 %copy.7.ids_ref = s32[8,2]{1,0:T(8,128)} copy(s32[8,2]{0,1:T(2,128)} %param.7) | data formatting | bytes 128 | tf_op args[1]
  1.3 1.3 %copy.8.gw_ref = f32[8,2]{1,0:T(8,128)} copy(f32[8,2]{0,1:T(2,128)} %param.8) | data formatting | bytes 128 | tf_op args[2]
  2.7 36.1 %shard_map.64 = bf16[8,3072]{1,0:T(8,128)(2,1)} custom-call(bf16[8,3072]{1,0:T(8,128)(2,1)} %tok_ref.1, s32[8,2]{1,0:T(8,128)} %copy.7.ids_ref, f32[8,2]{1,0:T(8,128)} %copy.8.gw_ref, bf16[1,3072,2048]{2,1,0:T(8,128)(2,1)} %gate_ref.1, bf16[1,3072,2048]{2,1,0:T(8,128)(2,1)} %up_ref.1, bf16[1,2048,3072]{2,1,0:T(8,128)(2,1)} %down_ref.1), custom_call_target="tpu_custom_call" | custom-call | tf_op jit(solution)/shard_map/pallas_call | solution.py:198
  38.8 1.4 %copy.10 = bf16[8,3072]{1,0:T(8,128)(2,1)} copy(bf16[8,3072]{1,0:T(8,128)(2,1)} %shard_map.64) | data formatting | bytes 98304

commit v2 on v1

v2 whole, which is shorter than its diff:
```python
import functools

import jax
import jax.numpy as jnp
from jax import lax
from jax.experimental import pallas as pl
from jax.experimental.pallas import tpu as pltpu
from jax.sharding import PartitionSpec as P

F32 = jnp.float32
BF16 = jnp.bfloat16
LANES = 128
DEPTH_MOST = 1536
F_MOST = 2048
MESH = pl.DeviceIdType.MESH


def chunk_width(total, most):
    width = most
    while total % width:
        width -= LANES
    return width


def layer(n_e, n_y, tok_ref, ids_ref, gw_ref, gate_ref, up_ref, down_ref, out_ref,
          xb, x, wts, gates, ups, hid, wg, wu, wd, part, core_in, mid, y_in, fin, z_in,
          tok_sem, g_sem, u_sem, d_sem,
          agz_s, agz_r, agy_s, agy_r, agc_s, agc_r,
          rc_s, rc_r, ry_s, ry_r, rz_s, rz_r):
    e = lax.axis_index("expert")
    t = lax.axis_index("tensor")
    y = t // 2
    c = t % 2
    rows, width = x.shape
    n_p, depth, ff = wg.shape
    f_w = chunk_width(ff, F_MOST)
    n_d, _, d_w = wd.shape

    def slot(cc, yy, ee):
        return (cc * n_y + yy) * n_e + ee

    me = slot(c, y, e)
    upper = e // (n_e // 2)
    mirrored = e + upper * (n_e - 1 - 2 * e)
    others_e = [j + (j + n_e - mirrored) // n_e for j in range(n_e - 1)]
    others_e = [q + upper * (n_e - 1 - 2 * q) for q in others_e]
    others_y = [(y + k) % n_y for k in range(1, n_y)]
    partner = {"tensor": y * 2 + 1 - c}

    tok = pltpu.make_async_copy(tok_ref, xb.at[me, :, pl.ds(0, width)], tok_sem)
    tok.start()
    barrier = pltpu.get_barrier_semaphore()
    pl.semaphore_signal(barrier, inc=1, device_id=partner, device_id_type=MESH)
    for yy in others_y:
        pl.semaphore_signal(barrier, inc=1, device_id={"tensor": yy * 2 + c}, device_id_type=MESH)
    for ee in others_e:
        pl.semaphore_signal(barrier, inc=1, device_id={"expert": ee}, device_id_type=MESH)

    lane = lax.broadcasted_iota(jnp.int32, (ids_ref.shape[1], LANES), 1)
    ids = ids_ref[...].T
    gw = gw_ref[...].T
    w = jnp.where(ids[:, 0:1] == lane, gw[:, 0:1], 0.0) + jnp.where(ids[:, 1:2] == lane, gw[:, 1:2], 0.0)
    head = w.astype(BF16)
    xb[me, :, pl.ds(width, LANES)] = head
    xb[me, :, pl.ds(width + LANES, LANES)] = (w - head.astype(F32)).astype(BF16)
    tok.wait()
    pl.semaphore_wait(barrier, 1 + len(others_y) + len(others_e))

    def gather(p, index, send, recv, device):
        at = xb.at[index, :, pl.ds(p * depth, depth + (2 * LANES if p == n_p - 1 else 0))]
        return pltpu.make_async_remote_copy(
            src_ref=at, dst_ref=at, send_sem=send.at[p], recv_sem=recv.at[p],
            device_id=device, device_id_type=MESH)

    sends = []

    def start(copy):
        copy.start()
        sends.append(copy)

    def gate_copy(p):
        return pltpu.make_async_copy(gate_ref.at[0, pl.ds(p * depth, depth), :], wg.at[p], g_sem.at[p])

    def up_copy(p):
        return pltpu.make_async_copy(up_ref.at[0, pl.ds(p * depth, depth), :], wu.at[p], u_sem.at[p])

    def down(i):
        return pltpu.make_async_copy(down_ref.at[0, :, pl.ds(i * d_w, d_w)], wd.at[i], d_sem.at[i])

    for p in range(n_p):
        for ee in others_e:
            start(gather(p, me, agz_s.at[ee], agz_r.at[e], {"expert": ee}))
        for m, yy in enumerate(others_y):
            start(gather(p, me, agy_s.at[m, e], agy_r.at[m, e], {"tensor": yy * 2 + c}))
        start(gather(p, me, agc_s.at[0, e], agc_r.at[0, e], partner))
    for p in range(n_p):
        gate_copy(p).start()
        up_copy(p).start()
    for i in range(n_d):
        down(i).start()

    def from_e(p):
        for ee in others_e:
            source = slot(c, y, ee)
            gather(p, source, agz_s.at[ee], agz_r.at[ee], partner).wait_recv()
            for m, yy in enumerate(others_y):
                start(gather(p, source, agy_s.at[m, ee], agy_r.at[m, ee], {"tensor": yy * 2 + c}))
            start(gather(p, source, agc_s.at[0, ee], agc_r.at[0, ee], partner))

    def from_y(p):
        for ee in [e] + others_e:
            for m in range(1, n_y):
                source = slot(c, (y + n_y - m) % n_y, ee)
                gather(p, source, agy_s.at[m - 1, ee], agy_r.at[m - 1, ee], partner).wait_recv()
                start(gather(p, source, agc_s.at[m, ee], agc_r.at[m, ee], partner))

    expert_lane = lax.broadcasted_iota(jnp.int32, (16, LANES), 1) == e

    def from_core(p):
        for ee in [e] + others_e:
            for m in range(n_y):
                source = slot(1 - c, (y + n_y - m) % n_y, ee)
                gather(p, source, agc_s.at[m, ee], agc_r.at[m, ee], partner).wait_recv()
        last = p == n_p - 1

        def gathered(j, carry):
            at = pl.ds(pl.multiple_of(16 * j, 16), 16)
            pair = xb[pl.ds(2 * j, 2), :, pl.ds(p * depth, depth)]
            x[at, pl.ds(p * depth, depth)] = pair.astype(F32).reshape(16, depth).astype(BF16)
            if last:
                both = xb[pl.ds(2 * j, 2), :, pl.ds(width, 2 * LANES)].astype(F32).reshape(16, 2 * LANES)
                own = jnp.where(expert_lane, both[:, :LANES] + both[:, LANES:], 0.0)
                wts[at, :] = jnp.broadcast_to(jnp.sum(own, axis=1, keepdims=True), (16, LANES))
            return carry

        lax.fori_loop(0, rows // 16, gathered, 0)
        gate_copy(p).wait()
        up_copy(p).wait()

        def columns(j, carry):
            at = pl.ds(pl.multiple_of(j * f_w, LANES), f_w)
            rows_in = x[:, pl.ds(p * depth, depth)]
            gate = jnp.dot(rows_in, wg[p, :, at], preferred_element_type=F32)
            up = jnp.dot(rows_in, wu[p, :, at], preferred_element_type=F32)
            if p > 0:
                gate = gate + gates[:, at]
                up = up + ups[:, at]
            if last:
                hid[:, at] = (gate / (1.0 + jnp.exp(-gate)) * up * wts[:, 0:1]).astype(BF16)
            else:
                gates[:, at] = gate
                ups[:, at] = up
            return carry

        lax.fori_loop(0, ff // f_w, columns, 0)

    for step in range(n_p + 3):
        for stage, lag in ((from_e, 0), (from_y, 1), (from_core, 2)):
            if 0 <= step - lag < n_p:
                stage(step - lag)

    def core_copy(i):
        return pltpu.make_async_remote_copy(
            src_ref=part.at[i, 1 - c], dst_ref=core_in.at[i], send_sem=rc_s.at[i], recv_sem=rc_r.at[i],
            device_id=partner, device_id_type=MESH)

    def y_copy(i, k, yy):
        return pltpu.make_async_remote_copy(
            src_ref=mid.at[i, yy], dst_ref=y_in.at[i, k], send_sem=ry_s.at[i, k], recv_sem=ry_r.at[i, k],
            device_id={"tensor": yy * 2 + c}, device_id_type=MESH)

    def z_copy(i, to, source):
        return pltpu.make_async_remote_copy(
            src_ref=fin.at[i, to], dst_ref=z_in.at[i, source], send_sem=rz_s.at[i, to],
            recv_sem=rz_r.at[i, source], device_id={"expert": to}, device_id_type=MESH)

    def produce(i):
        down(i).wait()
        value = jnp.dot(hid[...], wd[i], preferred_element_type=F32)
        part[i] = value.reshape(
            part.shape[1:]).astype(BF16)
        start(core_copy(i))

    def over_cores(i):
        core_copy(i).wait_recv()
        mid[i] = (part[i, c].astype(F32) + core_in[i].astype(F32)).astype(BF16)
        for k, yy in enumerate(others_y):
            start(y_copy(i, k, yy))

    def over_y(i):
        total = mid[i, y].astype(F32)
        for k, yy in enumerate(others_y):
            y_copy(i, k, yy).wait_recv()
            total = total + y_in[i, k].astype(F32)
        fin[i] = total.astype(BF16)
        for ee in reversed(others_e):
            start(z_copy(i, ee, e))

    def over_e(i):
        total = fin[i, e].astype(F32)
        for ee in others_e:
            z_copy(i, ee, ee).wait_recv()
            total = total + z_in[i, ee].astype(F32)
        out_ref[:, pl.ds(i * d_w, d_w)] = total.astype(BF16)

    lags = ((produce, 0), (over_cores, 1), (over_y, 5), (over_e, 11))
    for step in range(n_d + lags[-1][1]):
        for stage, lag in lags:
            if 0 <= step - lag < n_d:
                stage(step - lag)
    for copy in sends:
        copy.wait_send()


def on_device(tokens, expert_ids, gate_weights, gate_proj, up_proj, down_proj):
    n_e = lax.axis_size("expert")
    n_t = lax.axis_size("tensor")
    n_y = n_t // 2
    local, width = tokens.shape
    ff = gate_proj.shape[2]
    rows = n_e * n_t * local
    depth = chunk_width(width, DEPTH_MOST)
    d_w = chunk_width(width, 512)
    n_p, n_d = width // depth, width // d_w
    hbm = pl.BlockSpec(memory_space=pl.ANY)
    vmem = pl.BlockSpec(memory_space=pltpu.VMEM)
    dma = pltpu.SemaphoreType.DMA
    return pl.pallas_call(
        functools.partial(layer, n_e, n_y),
        out_shape=jax.ShapeDtypeStruct((local, width), BF16),
        in_specs=[hbm, vmem, vmem, hbm, hbm, hbm],
        out_specs=vmem,
        scratch_shapes=[
            pltpu.VMEM((n_e * n_t, local, width + 2 * LANES), BF16),
            pltpu.VMEM((rows, width), BF16),
            pltpu.VMEM((rows, LANES), F32),
            pltpu.VMEM((rows, ff), F32),
            pltpu.VMEM((rows, ff), F32),
            pltpu.VMEM((rows, ff), BF16),
            pltpu.VMEM((n_p, depth, ff), BF16),
            pltpu.VMEM((n_p, depth, ff), BF16),
            pltpu.VMEM((n_d, ff, d_w), BF16),
            pltpu.VMEM((n_d, 2, n_y, n_e, local, d_w), BF16),
            pltpu.VMEM((n_d, n_y, n_e, local, d_w), BF16),
            pltpu.VMEM((n_d, n_y, n_e, local, d_w), BF16),
            pltpu.VMEM((n_d, max(1, n_y - 1), n_e, local, d_w), BF16),
            pltpu.VMEM((n_d, n_e, local, d_w), BF16),
            pltpu.VMEM((n_d, n_e, local, d_w), BF16),
            dma, dma((n_p,)), dma((n_p,)), dma((n_d,)),
            dma((n_e, n_p)), dma((n_e, n_p)),
            dma((n_y, n_e, n_p)), dma((n_y, n_e, n_p)),
            dma((n_y, n_e, n_p)), dma((n_y, n_e, n_p)),
            dma((n_d,)), dma((n_d,)),
            dma((n_d, n_y)), dma((n_d, n_y)),
            dma((n_d, n_e)), dma((n_d, n_e)),
        ],
        compiler_params=pltpu.CompilerParams(
            collective_id=0, has_side_effects=True, vmem_limit_bytes=64000 * 1024),
    )(tokens, expert_ids.T, gate_weights.T, gate_proj, up_proj, down_proj)


def solution(mesh):
    return jax.shard_map(
        on_device,
        mesh=mesh,
        in_specs=(
            P(("dp", "expert", "tensor"), None),
            P(("dp", "expert", "tensor"), None),
            P(("dp", "expert", "tensor"), None),
            P("expert", None, "tensor"),
            P("expert", None, "tensor"),
            P("expert", "tensor", None),
        ),
        out_specs=P(("dp", "expert", "tensor"), None),
        check_vma=False,
    )
```

time: 40.5 us -> 34.9 us (0.86)
  Pallas kernels: 36.1 us -> 33.2 us
  local copies, waits for them, and re-layouts: 4.11 us -> 1.42 us
    pallas_call x1, Pallas kernels: 36.1 us -> 33.2 us  [on_device(): pl.pallas_call(functools.partial(layer, n_e, n_y), out_shape=jax.ShapeDty...]
    unnamed x3 -> x1, local copies, waits for them, and re-layouts: 4.11 us -> 1.42 us
where the time goes in v2:
time: 34.9 us; the launch traced here: 34.7 us
  Pallas kernels  33.2 us (95%)
  local copies, waits for them, and re-layouts  1.42 us (4%)
    pallas_call x1, Pallas kernels, on_device(): pl.pallas_call(functools.partial(layer, n_e, n_y), out_shape=jax.ShapeDty...  33.2 us
    unnamed x1, local copies, waits for them, and re-layouts  1.42 us

profile of v2, /device:TPU:0, one launch (start us, length us, event | category | flops | bytes accessed | tf_op | source)
XLA Modules:
  0.0 34.7 jit_solution(11364113830252128485)
XLA Ops:
  0.0 33.2 %shard_map.64 = bf16[8,3072]{1,0:T(8,128)(2,1)} custom-call(bf16[8,3072]{1,0:T(8,128)(2,1)} %tok_ref.1, s32[2,8]{1,0:T(2,128)} %bitcast.2, f32[2,8]{1,0:T(2,128)} %bitcast.3, bf16[1,3072,2048]{2,1,0:T(8,128)(2,1)} %gate_ref.1, bf16[1,3072,2048]{2,1,0:T(8,128)(2,1)} %up_ref.1, bf16[1,2048,3072]{2,1,0:T(8,128)(2,1)} %down_ref.1), custom_call_target="tpu_custom_call" | custom-call | tf_op jit(solution)/shard_map/pallas_call | solution.py:228
  33.2 1.4 %copy.8 = bf16[8,3072]{1,0:T(8,128)(2,1)} copy(bf16[8,3072]{1,0:T(8,128)(2,1)} %shard_map.64) | data formatting | bytes 98304
